TPU v7x, 32 devices: a whole 2x2x4 slice. The times are simulated.
32 devices in a mesh: dom: 32 (over z, y, x, core).
Axes of the slice: x: 2, y: 2, z: 4, core: 2. Of those that a mesh axis runs over, the one named last changes fastest.
Arguments:
- node_emb: bfloat16 [16384, 64], P('dom'), may hold values from -6 to 6
- hub_emb: bfloat16 [256, 64], replicated, may hold values from -6 to 6
- tile_vals: bfloat16 [4096, 128, 128], P('dom')
- tile_col: int32 [4096], P('dom'), may hold values from 0 to 5
- tile_dest: int32 [4096], P('dom'), may hold values from 0 to 29, as said below
Outputs:
- node_out: float32 [16384, 64], P('dom')
- hub_out: float32 [256, 64], replicated
Inputs may be any that keep to these rules, and one draw needn't show every extreme that they name: tile_dest below 28 names a partition offset from -3 to 3 and a block of that partition; from 28 up it names a hub block. tile_col below 4 names one of the holding partition's own blocks; from 4 up it names a hub block.
All inputs are finite; a program needn't handle non-finite values.
Results may differ from a plain program's by a relative error of at most 0.0003.
Values sent between devices are 32-bit elements.
A program may use at most 64 MiB of HBM per device.

v0:
```python
import jax
import jax.numpy as jnp
from jax import lax
from jax.sharding import PartitionSpec as P

REACH_BITS = 2
LAYERS = 2


def shifted(block, axis, distance):
    devices = range(lax.axis_size(axis))
    route = [((i - distance) % len(devices), i) for i in devices]
    return lax.ppermute(block, axis, route)


def route_partials(spread, farthest):
    overall = spread[farthest]
    for heading in (1, -1):
        for distance in range(1, farthest + 1):
            overall = overall + shifted(
                spread[farthest + heading * distance], "dom", heading * distance
            )
    return overall


def shards(node_emb, hub_emb, tile_vals, tile_col, tile_dest):
    tile_size = tile_vals.shape[1]
    features = node_emb.shape[1]
    dev_rows = node_emb.shape[0]
    own_blocks = dev_rows // tile_size
    hub_rows = hub_emb.shape[0]
    hub_blocks = hub_rows // tile_size
    tile_count = tile_vals.shape[0]
    farthest = 2**REACH_BITS - 1
    slot_count = 2 * farthest + 1
    target_count = slot_count * own_blocks + hub_blocks
    one_hot = (tile_dest[None, :] == jnp.arange(target_count, dtype=jnp.int32)[:, None]).astype(
        jnp.float32
    )
    current_node = node_emb
    current_hub = hub_emb
    node_total = node_emb.astype(jnp.float32)
    hub_total = hub_emb.astype(jnp.float32)
    for layer_index in range(LAYERS):
        sources = jnp.concatenate([current_node, current_hub], 0).reshape(
            own_blocks + hub_blocks, tile_size, features
        )
        picked = jnp.take(sources, tile_col, axis=0)
        products = jnp.einsum("tij,tjd->tid", tile_vals, picked, preferred_element_type=jnp.float32)
        summed = jnp.dot(
            one_hot,
            products.reshape(tile_count, tile_size * features),
            precision=lax.Precision.HIGHEST,
            preferred_element_type=jnp.float32,
        )
        spread = summed[: slot_count * own_blocks].reshape(slot_count, dev_rows, features)
        hub_part = summed[slot_count * own_blocks :].reshape(hub_rows, features)
        hub_sum = lax.psum(hub_part, "dom")
        node_sum = route_partials(spread, farthest)
        node_total = node_total + node_sum
        hub_total = hub_total + hub_sum
        current_node = node_sum.astype(jnp.bfloat16)
        current_hub = hub_sum.astype(jnp.bfloat16)
    return (node_total / float(LAYERS + 1), hub_total / float(LAYERS + 1))


def solution(mesh):
    in_specs = (P("dom", None), P(), P("dom", None, None), P("dom"), P("dom"))
    out_specs = (P("dom", None), P())
    return jax.shard_map(shards, mesh=mesh, in_specs=in_specs, out_specs=out_specs, check_vma=False)
```

profile of v0, /device:TPU:0, one launch (start us, length us, event | category | flops | bytes accessed | tf_op | source)
XLA Modules:
  0.0 331.4 jit_solution(637796549837110401)
XLA Ops:
  7.2 0.0 all-reduce.3.cloned.1.call-start
  7.2 0.7 compare_select_fusion
  7.9 0.7 compare_and_fusion
  8.5 0.9 copy_bitcast_fusion
  9.4 1.0 gather_fusion
  10.4 7.1 %convolution_bitcast_fusion.1 = f32[128,128,64]{1,2,0:T(8,128)} fusion(bf16[128,128,128]{2,1,0:T(8,128)(2,1)} %param.9, bf16[128,128,64]{1,2,0:T(8,128)(2,1)S(1)} %gather_fusion, pred[128]{0:T(512)(128)(4,1)S(1)} %compare_and_fusion), kind=kOutput, calls=%fused_computation.3 | convolution fusion | flops 269484032 | bytes 10485888 | tf_op jit(solution)/shard_map/tij,tjd->tid/dot_general | solution.py:49
  17.5 5.5 %copy.25 = f32[128,128,64]{0,2,1:T(8,128)} copy(f32[128,128,64]{1,2,0:T(8,128)} %convolution_bitcast_fusion.1) | data formatting | bytes 8388608 | tf_op jit(solution)/shard_map/tij,tjd->tid/dot_general | solution.py:49
  22.9 4.6 %fusion.7 = f32[30,8192]{1,0:T(8,128)S(1)} fusion(f32[128,8192]{0,1:T(8,128)} %bitcast.16, s32[128]{0:T(128)S(1)} %copy-done.3), kind=kOutput, calls=%fused_computation.18 | convolution fusion | flops 377491200 | bytes 5177856 | tf_op jit(solution)/shard_map/dot_general | solution.py:50
  27.5 0.1 fusion.14
  27.7 0.2 squeeze.43
  27.8 0.5 collective-permute-start
  28.4 0.2 squeeze.44
  28.5 2.5 collective-permute-start.1
  31.1 0.2 squeeze.45
  31.3 2.4 collective-permute-start.2
  33.7 0.9 squeeze.46
  34.6 3.0 collective-permute-start.3
  37.5 0.9 squeeze.47
  38.4 1.2 collective-permute-start.4
  39.6 0.9 squeeze.48
  40.5 2.4 collective-permute-done
  42.9 0.0 collective-permute-start.5
  42.9 0.8 reshape.60
  43.7 0.0 all-reduce.3.cloned.1.call-update
  43.7 0.2 all-reduce.5.cloned.1.call-start
  43.9 0.2 squeeze.42
  44.1 124.6 %all-reduce.3.cloned.1.call-done = f32[256,64]{1,0:T(8,128)} async-done(((f32[256,64]{1,0:T(8,128)}), f32[256,64]{1,0:T(8,128)}) %all-reduce.3.cloned.1.call-update) | async-done | bytes 65552 | tf_op jit(solution)/shard_map/psum | solution.py:58
  168.7 0.9 convert_element_type.15
  169.6 0.0 collective-permute-done.1
  169.6 0.0 collective-permute-done.2
  169.6 0.0 collective-permute-done.3
  169.6 0.0 collective-permute-done.5
  169.6 0.1 fusion.12
  169.8 0.1 copy.27
  169.9 1.0 gather_fusion.1
  170.9 7.1 %convolution_bitcast_fusion = f32[128,128,64]{1,2,0:T(8,128)} fusion(bf16[128,128,128]{2,1,0:T(8,128)(2,1)} %param.9, bf16[128,128,64]{1,2,0:T(8,128)(2,1)S(1)} %gather_fusion.1, pred[128]{0:T(512)(128)(4,1)S(1)} %compare_and_fusion), kind=kOutput, calls=%fused_computation.2 | convolution fusion | flops 269484032 | bytes 10485888 | tf_op jit(solution)/shard_map/tij,tjd->tid/dot_general | solution.py:49
  178.0 5.4 %copy.28 = f32[128,128,64]{0,2,1:T(8,128)} copy(f32[128,128,64]{1,2,0:T(8,128)} %convolution_bitcast_fusion) | data formatting | bytes 8388608 | tf_op jit(solution)/shard_map/tij,tjd->tid/dot_general | solution.py:49
  183.4 4.6 %fusion.6 = f32[30,8192]{1,0:T(8,128)S(1)} fusion(f32[128,8192]{0,1:T(8,128)} %bitcast.17, s32[128]{0:T(128)S(1)} %copy-done.3), kind=kOutput, calls=%fused_computation.17 | convolution fusion | flops 377491200 | bytes 5177856 | tf_op jit(solution)/shard_map/dot_general | solution.py:50
  188.1 0.1 fusion.13
  188.2 0.2 squeeze.54
  188.4 3.3 collective-permute-start.10
  191.7 0.8 reshape.63
  192.5 0.0 all-reduce.5.cloned.1.call-update
  192.5 0.1 copy.23
  192.7 0.1 copy.29
  192.8 0.2 squeeze.55
  193.0 0.0 collective-permute-start.11
  193.0 0.9 squeeze.50
  193.9 1.6 collective-permute-start.6
  195.5 0.9 squeeze.51
  196.4 0.6 collective-permute-start.7
  196.9 0.9 squeeze.52
  197.8 0.9 squeeze.53
  198.7 0.2 squeeze.49
  198.9 0.8 collective-permute-done.10
  199.7 3.6 %collective-permute-start.9 = (f32[512,64]{1,0:T(8,128)}, f32[512,64]{1,0:T(8,128)S(1)}, u32[]{:S(2)}, u32[]{:S(2)}) collective-permute-start(f32[512,64]{1,0:T(8,128)} %squeeze.53), channel_id=1, source_target_pairs={{1,0},{2,1},{3,2},{4,3},{5,4},{6,5},{7,6},{8,7},{9,8},{10,9},{11,1... | collective-permute-start | bytes 393224 | tf_op jit(solution)/shard_map/ppermute | solution.py:13
  203.3 118.6 %all-reduce.5.cloned.1.call-done = f32[256,64]{1,0:T(8,128)} async-done(((f32[256,64]{1,0:T(8,128)}), f32[256,64]{1,0:T(8,128)}) %all-reduce.5.cloned.1.call-update) | async-done | bytes 65552 | tf_op jit(solution)/shard_map/psum | solution.py:58
  321.9 0.9 add_multiply_fusion.1
  322.9 0.7 copy.31
  323.6 0.0 collective-permute-done.11
  323.6 0.0 collective-permute-done.6
  323.6 0.0 collective-permute-done.8
  323.6 0.1 add_multiply_fusion
  323.7 0.8 copy.30
  (16 shorter events, 0.1 us)
Async XLA Ops:
  7.2 161.5 %all-reduce.3.cloned.1.call-start = ((), (), s32[]{:S(2)}) async-start(), calls=%async_computation | async-start | bytes 262144 | tf_op jit(solution)/shard_map/psum | solution.py:58
  17.5 5.5 %copy-start.3 = (s32[128]{0:T(128)S(1)}, s32[128]{0:T(128)}, u32[]{:S(2)}) copy-start(s32[128]{0:T(128)} %param.11) | copy-start | bytes 1540
  27.8 15.0 %collective-permute-start = (f32[512,64]{1,0:T(8,128)S(1)}, f32[512,64]{1,0:T(8,128)S(1)}, u32[]{:S(2)}, u32[]{:S(2)}) collective-permute-start(f32[512,64]{1,0:T(8,128)S(1)} %squeeze.43), channel_id=1, source_target_pairs={{31,0},{0,1},{1,2},{2,3},{3,4},{4,5},{5,6},{6,7},{7,8},{8,9},{9,10... | collective-permute-start | bytes 393224 | tf_op jit(solution)/shard_map/ppermute | solution.py:13
  28.5 141.1 %collective-permute-start.1 = (f32[512,64]{1,0:T(8,128)S(1)}, f32[512,64]{1,0:T(8,128)S(1)}, u32[]{:S(2)}, u32[]{:S(2)}) collective-permute-start(f32[512,64]{1,0:T(8,128)S(1)} %squeeze.44), channel_id=1, source_target_pairs={{30,0},{31,1},{0,2},{1,3},{2,4},{3,5},{4,6},{5,7},{6,8},{7,9},{8,1... | collective-permute-start | bytes 393224 | tf_op jit(solution)/shard_map/ppermute | solution.py:13
  31.3 138.4 %collective-permute-start.2 = (f32[512,64]{1,0:T(8,128)S(1)}, f32[512,64]{1,0:T(8,128)S(1)}, u32[]{:S(2)}, u32[]{:S(2)}) collective-permute-start(f32[512,64]{1,0:T(8,128)S(1)} %squeeze.45), channel_id=1, source_target_pairs={{29,0},{30,1},{31,2},{0,3},{1,4},{2,5},{3,6},{4,7},{5,8},{6,9},{7,... | collective-permute-start | bytes 393224 | tf_op jit(solution)/shard_map/ppermute | solution.py:13
  34.6 135.0 %collective-permute-start.3 = (f32[512,64]{1,0:T(8,128)}, f32[512,64]{1,0:T(8,128)S(1)}, u32[]{:S(2)}, u32[]{:S(2)}) collective-permute-start(f32[512,64]{1,0:T(8,128)} %squeeze.46), channel_id=1, source_target_pairs={{1,0},{2,1},{3,2},{4,3},{5,4},{6,5},{7,6},{8,7},{9,8},{10,9},{11,1... | collective-permute-start | bytes 393224 | tf_op jit(solution)/shard_map/ppermute | solution.py:13
  38.4 131.2 %collective-permute-start.4 = (f32[512,64]{1,0:T(8,128)}, f32[512,64]{1,0:T(8,128)S(1)}, u32[]{:S(2)}, u32[]{:S(2)}) collective-permute-start(f32[512,64]{1,0:T(8,128)} %squeeze.47), channel_id=1, source_target_pairs={{2,0},{3,1},{4,2},{5,3},{6,4},{7,5},{8,6},{9,7},{10,8},{11,9},{12,... | collective-permute-start | bytes 393224 | tf_op jit(solution)/shard_map/ppermute | solution.py:13
  42.9 126.8 %collective-permute-start.5 = (f32[512,64]{1,0:T(8,128)}, f32[512,64]{1,0:T(8,128)S(1)}, u32[]{:S(2)}, u32[]{:S(2)}) collective-permute-start(f32[512,64]{1,0:T(8,128)} %squeeze.48), channel_id=1, source_target_pairs={{3,0},{4,1},{5,2},{6,3},{7,4},{8,5},{9,6},{10,7},{11,8},{12,9},{13... | collective-permute-start | bytes 393224 | tf_op jit(solution)/shard_map/ppermute | solution.py:13
  43.7 278.2 %all-reduce.5.cloned.1.call-start = ((), (), s32[]{:S(2)}) async-start(), calls=%async_computation.1 | async-start | bytes 262144 | tf_op jit(solution)/shard_map/psum | solution.py:58
  183.4 9.1 %copy-start.1 = (bf16[512,64]{0,1:T(8,128)(2,1)S(1)}, bf16[512,64]{0,1:T(8,128)(2,1)}, u32[]{:S(2)}) copy-start(bf16[512,64]{0,1:T(8,128)(2,1)} %param.7) | copy-start | bytes 196612
  183.4 9.2 %copy-start.2 = (bf16[256,64]{0,1:T(8,128)(2,1)S(1)}, bf16[256,64]{0,1:T(8,128)(2,1)}, u32[]{:S(2)}) copy-start(bf16[256,64]{0,1:T(8,128)(2,1)} %param.8) | copy-start | bytes 98308
  183.4 138.5 %copy-start = (f32[256,64]{1,0:T(8,128)S(1)}, f32[256,64]{1,0:T(8,128)}, u32[]{:S(2)}) copy-start(f32[256,64]{1,0:T(8,128)} %all-reduce.3.cloned.1.call-done) | copy-start | bytes 196612
  188.4 11.3 %collective-permute-start.10 = (f32[512,64]{1,0:T(8,128)S(1)}, f32[512,64]{1,0:T(8,128)S(1)}, u32[]{:S(2)}, u32[]{:S(2)}) collective-permute-start(f32[512,64]{1,0:T(8,128)S(1)} %squeeze.54), channel_id=1, source_target_pairs={{2,0},{3,1},{4,2},{5,3},{6,4},{7,5},{8,6},{9,7},{10,8},{11,9},{12,... | collective-permute-start | bytes 393224 | tf_op jit(solution)/shard_map/ppermute | solution.py:13
  193.0 130.6 %collective-permute-start.11 = (f32[512,64]{1,0:T(8,128)S(1)}, f32[512,64]{1,0:T(8,128)S(1)}, u32[]{:S(2)}, u32[]{:S(2)}) collective-permute-start(f32[512,64]{1,0:T(8,128)S(1)} %squeeze.55), channel_id=1, source_target_pairs={{3,0},{4,1},{5,2},{6,3},{7,4},{8,5},{9,6},{10,7},{11,8},{12,9},{13... | collective-permute-start | bytes 393224 | tf_op jit(solution)/shard_map/ppermute | solution.py:13
  193.9 129.7 %collective-permute-start.6 = (f32[512,64]{1,0:T(8,128)}, f32[512,64]{1,0:T(8,128)S(1)}, u32[]{:S(2)}, u32[]{:S(2)}) collective-permute-start(f32[512,64]{1,0:T(8,128)} %squeeze.50), channel_id=1, source_target_pairs={{31,0},{0,1},{1,2},{2,3},{3,4},{4,5},{5,6},{6,7},{7,8},{8,9},{9,10... | collective-permute-start | bytes 393224 | tf_op jit(solution)/shard_map/ppermute | solution.py:13
  196.4 127.2 %collective-permute-start.7 = (f32[512,64]{1,0:T(8,128)}, f32[512,64]{1,0:T(8,128)S(1)}, u32[]{:S(2)}, u32[]{:S(2)}) collective-permute-start(f32[512,64]{1,0:T(8,128)} %squeeze.51), channel_id=1, source_target_pairs={{30,0},{31,1},{0,2},{1,3},{2,4},{3,5},{4,6},{5,7},{6,8},{7,9},{8,1... | collective-permute-start | bytes 393224 | tf_op jit(solution)/shard_map/ppermute | solution.py:13
  197.8 125.8 %collective-permute-start.8 = (f32[512,64]{1,0:T(8,128)}, f32[512,64]{1,0:T(8,128)S(1)}, u32[]{:S(2)}, u32[]{:S(2)}) collective-permute-start(f32[512,64]{1,0:T(8,128)} %squeeze.52), channel_id=1, source_target_pairs={{29,0},{30,1},{31,2},{0,3},{1,4},{2,5},{3,6},{4,7},{5,8},{6,9},{7,... | collective-permute-start | bytes 393224 | tf_op jit(solution)/shard_map/ppermute | solution.py:13
  199.7 123.9 %collective-permute-start.9 = (f32[512,64]{1,0:T(8,128)}, f32[512,64]{1,0:T(8,128)S(1)}, u32[]{:S(2)}, u32[]{:S(2)}) collective-permute-start(f32[512,64]{1,0:T(8,128)} %squeeze.53), channel_id=1, source_target_pairs={{1,0},{2,1},{3,2},{4,3},{5,4},{6,5},{7,6},{8,7},{9,8},{10,9},{11,1... | collective-permute-start | bytes 393224 | tf_op jit(solution)/shard_map/ppermute | solution.py:13
Sparse Core Ops, SparseCore 0:
  43.8 124.8 all-reduce.2
  192.7 129.2 all-reduce.4
where the time goes:
time: 332 us; the launch traced here: 331 us
  waiting for transfers between devices  246 us (74%)
  local copies, waits for them, and re-layouts  24.1 us (7%)
  matrix products  23.3 us (7%)
  starting transfers between devices  19 us (6%)
  between operations  14.2 us (4%)
  other arithmetic  4.29 us (1%)
    psum x2, waiting for transfers between devices, shards(): hub_sum = lax.psum(hub_part, 'dom')  243 us
    ppermute x12, starting transfers between devices, shifted(): return lax.ppermute(block, axis, route)  18.7 us
    dot_general x2, matrix products, shards(): jnp.einsum('tij,tjd->tid', tile_vals, picked, preferred_element_type=jnp....  14.1 us
    dot_general x2, local copies, waits for them, and re-layouts, shards(): jnp.einsum('tij,tjd->tid', tile_vals, picked, preferred_element_type=jnp....  10.9 us
    dot_general x2, matrix products, shards(): jnp.dot(one_hot, products.reshape(tile_count, tile_size * features), prec...  9.19 us
    squeeze x12, local copies, waits for them, and re-layouts, route_partials(): spread[farthest + heading * distance]  7.08 us
  transfers between devices with their start and end apart: 14, of which 4 were waited for; matrix products, arithmetic and copies ran while one was open for 3% of the time, Pallas kernels for 0%

commit v1 on v0

--- a/solution.py
+++ b/solution.py
@@ -55,7 +55,7 @@
         )
         spread = summed[: slot_count * own_blocks].reshape(slot_count, dev_rows, features)
         hub_part = summed[slot_count * own_blocks :].reshape(hub_rows, features)
-        hub_sum = lax.psum(hub_part, "dom")
+        hub_sum = jax.lax.all_gather(hub_part, "dom").sum(axis=0)
         node_sum = route_partials(spread, farthest)
         node_total = node_total + node_sum
         hub_total = hub_total + hub_sum

time: 332 us -> 197 us (0.59)
  waiting for transfers between devices: 246 us -> 109 us
    psum x2 -> x0, waiting for transfers between devices: 243 us -> none  [shards(): hub_sum = lax.psum(hub_part, 'dom')]
    all_gather x0 -> x2, waiting for transfers between devices: none -> 80.9 us  [shards(): hub_sum = jax.lax.all_gather(hub_part, 'dom').sum(axis=0)]
    ppermute x12, waiting for transfers between devices: 3.24 us -> 28.4 us  [shifted(): return lax.ppermute(block, axis, route)]
    reduce_sum x0 -> x2, other arithmetic: none -> 3.43 us  [shards(): hub_sum = jax.lax.all_gather(hub_part, 'dom').sum(axis=0)]
  transfers between devices with their start and end apart: 14 -> 14, of which waited for: 4 -> 10; matrix products, arithmetic and copies ran while one was open for 3% -> 3% of each run, Pallas kernels for 0% -> 0%
where the time goes in v1:
time: 197 us; the launch traced here: 196 us
  waiting for transfers between devices  109 us (55%)
  matrix products  23.3 us (12%)
  local copies, waits for them, and re-layouts  21.5 us (11%)
  starting transfers between devices  21.1 us (11%)
  between operations  14.2 us (7%)
  other arithmetic  6.53 us (3%)
    all_gather x2, waiting for transfers between devices, shards(): hub_sum = jax.lax.all_gather(hub_part, 'dom').sum(axis=0)  80.9 us
    ppermute x12, waiting for transfers between devices, shifted(): return lax.ppermute(block, axis, route)  28.4 us
    ppermute x12, starting transfers between devices, shifted(): return lax.ppermute(block, axis, route)  21.1 us
    dot_general x2, matrix products, shards(): jnp.einsum('tij,tjd->tid', tile_vals, picked, preferred_element_type=jnp....  14.2 us
    dot_general x2, local copies, waits for them, and re-layouts, shards(): jnp.einsum('tij,tjd->tid', tile_vals, picked, preferred_element_type=jnp....  11 us
    dot_general x2, matrix products, shards(): jnp.dot(one_hot, products.reshape(tile_count, tile_size * features), prec...  9.19 us
    squeeze x12, local copies, waits for them, and re-layouts, route_partials(): spread[farthest + heading * distance]  5.07 us
  transfers between devices with their start and end apart: 14, of which 10 were waited for; matrix products, arithmetic and copies ran while one was open for 3% of the time, Pallas kernels for 0%

profile of v1, /device:TPU:0, one launch (start us, length us, event | category | flops | bytes accessed | tf_op | source)
XLA Modules:
  0.0 196.1 jit_solution(5008848456689445085)
XLA Ops:
  7.2 0.0 all-gather.3.cloned.1.call-start
  7.2 0.7 compare_select_fusion
  7.9 0.7 compare_and_fusion
  8.5 0.9 copy_bitcast_fusion
  9.4 1.0 gather_fusion
  10.4 7.1 %convolution_bitcast_fusion.1 = f32[128,128,64]{1,2,0:T(8,128)} fusion(bf16[128,128,128]{2,1,0:T(8,128)(2,1)} %param.9, bf16[128,128,64]{1,2,0:T(8,128)(2,1)S(1)} %gather_fusion, pred[128]{0:T(512)(128)(4,1)S(1)} %compare_and_fusion), kind=kOutput, calls=%fused_computation.3 | convolution fusion | flops 269484032 | bytes 10485888 | tf_op jit(solution)/shard_map/tij,tjd->tid/dot_general | solution.py:49
  17.5 5.5 %copy.43 = f32[128,128,64]{0,2,1:T(8,128)} copy(f32[128,128,64]{1,2,0:T(8,128)} %convolution_bitcast_fusion.1) | data formatting | bytes 8388608 | tf_op jit(solution)/shard_map/tij,tjd->tid/dot_general | solution.py:49
  23.0 4.6 %fusion.7 = f32[30,8192]{1,0:T(8,128)S(1)} fusion(f32[128,8192]{0,1:T(8,128)} %bitcast.16, s32[128]{0:T(128)S(1)} %copy-done.2), kind=kOutput, calls=%fused_computation.18 | convolution fusion | flops 377491200 | bytes 5177856 | tf_op jit(solution)/shard_map/dot_general | solution.py:50
  27.6 0.1 all_gather_reshape.6
  27.7 0.7 copy.44
  28.4 0.0 all-gather.3.cloned.1.call-update
  28.5 0.0 all-gather.5.cloned.1.call-start
  28.5 0.1 fusion.14
  28.7 0.2 squeeze.43
  28.8 0.5 collective-permute-start
  29.4 0.2 squeeze.44
  29.5 2.5 %collective-permute-start.1 = (f32[512,64]{1,0:T(8,128)S(1)}, f32[512,64]{1,0:T(8,128)S(1)}, u32[]{:S(2)}, u32[]{:S(2)}) collective-permute-start(f32[512,64]{1,0:T(8,128)S(1)} %squeeze.44), channel_id=1, source_target_pairs={{30,0},{31,1},{0,2},{1,3},{2,4},{3,5},{4,6},{5,7},{6,8},{7,9},{8,1... | collective-permute-start | bytes 393224 | tf_op jit(solution)/shard_map/ppermute | solution.py:13
  32.1 0.2 squeeze.45
  32.3 2.4 %collective-permute-start.2 = (f32[512,64]{1,0:T(8,128)S(1)}, f32[512,64]{1,0:T(8,128)S(1)}, u32[]{:S(2)}, u32[]{:S(2)}) collective-permute-start(f32[512,64]{1,0:T(8,128)S(1)} %squeeze.45), channel_id=1, source_target_pairs={{29,0},{30,1},{31,2},{0,3},{1,4},{2,5},{3,6},{4,7},{5,8},{6,9},{7,... | collective-permute-start | bytes 393224 | tf_op jit(solution)/shard_map/ppermute | solution.py:13
  34.7 0.2 squeeze.46
  34.9 3.0 %collective-permute-start.3 = (f32[512,64]{1,0:T(8,128)S(1)}, f32[512,64]{1,0:T(8,128)S(1)}, u32[]{:S(2)}, u32[]{:S(2)}) collective-permute-start(f32[512,64]{1,0:T(8,128)S(1)} %squeeze.46), channel_id=1, source_target_pairs={{1,0},{2,1},{3,2},{4,3},{5,4},{6,5},{7,6},{8,7},{9,8},{10,9},{11,1... | collective-permute-start | bytes 393224 | tf_op jit(solution)/shard_map/ppermute | solution.py:13
  37.9 0.2 squeeze.47
  38.1 1.2 collective-permute-start.4
  39.3 0.9 squeeze.48
  40.2 3.8 %collective-permute-done = f32[512,64]{1,0:T(8,128)S(1)} collective-permute-done((f32[512,64]{1,0:T(8,128)S(1)}, f32[512,64]{1,0:T(8,128)S(1)}, u32[]{:S(2)}, u32[]{:S(2)}) %collective-permute-start) | collective-permute-done | bytes 131104 | tf_op jit(solution)/shard_map/ppermute | solution.py:13
  44.0 0.2 squeeze.42
  44.1 2.0 %collective-permute-done.1 = f32[512,64]{1,0:T(8,128)S(1)} collective-permute-done((f32[512,64]{1,0:T(8,128)S(1)}, f32[512,64]{1,0:T(8,128)S(1)}, u32[]{:S(2)}, u32[]{:S(2)}) %collective-permute-start.1) | collective-permute-done | bytes 131104 | tf_op jit(solution)/shard_map/ppermute | solution.py:13
  46.1 9.2 %collective-permute-done.2 = f32[512,64]{1,0:T(8,128)S(1)} collective-permute-done((f32[512,64]{1,0:T(8,128)S(1)}, f32[512,64]{1,0:T(8,128)S(1)}, u32[]{:S(2)}, u32[]{:S(2)}) %collective-permute-start.2) | collective-permute-done | bytes 131104 | tf_op jit(solution)/shard_map/ppermute | solution.py:13
  55.3 2.0 %collective-permute-done.4 = f32[512,64]{1,0:T(8,128)S(1)} collective-permute-done((f32[512,64]{1,0:T(8,128)S(1)}, f32[512,64]{1,0:T(8,128)S(1)}, u32[]{:S(2)}, u32[]{:S(2)}) %collective-permute-start.4) | collective-permute-done | bytes 131104 | tf_op jit(solution)/shard_map/ppermute | solution.py:13
  57.3 0.1 fusion.12
  57.4 41.3 %all-gather.3.cloned.1.call-done = f32[32,256,64]{1,2,0:T(8,128)} async-done(((f32[1,256,64]{1,2,0:T(8,128)}), f32[32,256,64]{1,2,0:T(8,128)}) %all-gather.3.cloned.1.call-update) | async-done | bytes 2097168 | tf_op jit(solution)/shard_map/all_gather | solution.py:58
  98.6 1.7 reduce_sum.18
  100.4 0.1 copy.45
  100.5 0.1 copy.47
  100.7 1.0 gather_fusion.1
  101.7 7.1 %convolution_bitcast_fusion = f32[128,128,64]{1,2,0:T(8,128)} fusion(bf16[128,128,128]{2,1,0:T(8,128)(2,1)} %param.9, bf16[128,128,64]{1,2,0:T(8,128)(2,1)S(1)} %gather_fusion.1, pred[128]{0:T(512)(128)(4,1)S(1)} %compare_and_fusion), kind=kOutput, calls=%fused_computation.2 | convolution fusion | flops 269484032 | bytes 10485888 | tf_op jit(solution)/shard_map/tij,tjd->tid/dot_general | solution.py:49
  108.7 5.5 %copy.48 = f32[128,128,64]{0,2,1:T(8,128)} copy(f32[128,128,64]{1,2,0:T(8,128)} %convolution_bitcast_fusion) | data formatting | bytes 8388608 | tf_op jit(solution)/shard_map/tij,tjd->tid/dot_general | solution.py:49
  114.2 4.6 %fusion.6 = f32[30,8192]{1,0:T(8,128)S(1)} fusion(f32[128,8192]{0,1:T(8,128)} %bitcast.17, s32[128]{0:T(128)S(1)} %copy-done.2), kind=kOutput, calls=%fused_computation.17 | convolution fusion | flops 377491200 | bytes 5177856 | tf_op jit(solution)/shard_map/dot_general | solution.py:50
  118.9 0.1 all_gather_reshape.7
  119.0 0.7 copy.49
  119.7 0.1 fusion.13
  119.9 0.2 squeeze.54
  120.1 3.1 %collective-permute-start.10 = (f32[512,64]{1,0:T(8,128)S(1)}, f32[512,64]{1,0:T(8,128)S(1)}, u32[]{:S(2)}, u32[]{:S(2)}) collective-permute-start(f32[512,64]{1,0:T(8,128)S(1)} %squeeze.54), channel_id=1, source_target_pairs={{2,0},{3,1},{4,2},{5,3},{6,4},{7,5},{8,6},{9,7},{10,8},{11,9},{12,... | collective-permute-start | bytes 393224 | tf_op jit(solution)/shard_map/ppermute | solution.py:13
  123.2 0.2 squeeze.55
  123.4 1.0 collective-permute-start.11
  124.4 0.2 squeeze.50
  124.6 0.6 collective-permute-start.6
  125.2 0.9 squeeze.51
  126.1 0.6 collective-permute-start.7
  126.7 0.9 squeeze.52
  127.6 0.6 collective-permute-start.8
  128.2 0.9 squeeze.53
  129.1 2.4 %collective-permute-done.10 = f32[512,64]{1,0:T(8,128)S(1)} collective-permute-done((f32[512,64]{1,0:T(8,128)S(1)}, f32[512,64]{1,0:T(8,128)S(1)}, u32[]{:S(2)}, u32[]{:S(2)}) %collective-permute-start.10) | collective-permute-done | bytes 131104 | tf_op jit(solution)/shard_map/ppermute | solution.py:13
  131.5 5.4 %collective-permute-start.9 = (f32[512,64]{1,0:T(8,128)}, f32[512,64]{1,0:T(8,128)S(1)}, u32[]{:S(2)}, u32[]{:S(2)}) collective-permute-start(f32[512,64]{1,0:T(8,128)} %squeeze.53), channel_id=1, source_target_pairs={{1,0},{2,1},{3,2},{4,3},{5,4},{6,5},{7,6},{8,7},{9,8},{10,9},{11,1... | collective-permute-start | bytes 393224 | tf_op jit(solution)/shard_map/ppermute | solution.py:13
  136.9 0.1 copy.41
  137.0 0.2 squeeze.49
  137.2 0.4 collective-permute-done.11
  137.7 4.4 %collective-permute-done.7 = f32[512,64]{1,0:T(8,128)S(1)} collective-permute-done((f32[512,64]{1,0:T(8,128)}, f32[512,64]{1,0:T(8,128)S(1)}, u32[]{:S(2)}, u32[]{:S(2)}) %collective-permute-start.7) | collective-permute-done | bytes 131104 | tf_op jit(solution)/shard_map/ppermute | solution.py:13
  142.1 4.2 %collective-permute-done.8 = f32[512,64]{1,0:T(8,128)S(1)} collective-permute-done((f32[512,64]{1,0:T(8,128)}, f32[512,64]{1,0:T(8,128)S(1)}, u32[]{:S(2)}, u32[]{:S(2)}) %collective-permute-start.8) | collective-permute-done | bytes 131104 | tf_op jit(solution)/shard_map/ppermute | solution.py:13
  146.3 0.1 add_multiply_fusion
  146.4 0.8 copy.50
  147.2 39.7 %all-gather.5.cloned.1.call-done = f32[32,256,64]{1,2,0:T(8,128)} async-done(((f32[1,256,64]{1,2,0:T(8,128)}), f32[32,256,64]{1,2,0:T(8,128)}) %all-gather.5.cloned.1.call-update) | async-done | bytes 2097168 | tf_op jit(solution)/shard_map/all_gather | solution.py:58
  186.8 1.7 reduce_sum.19
  188.6 0.6 add_multiply_fusion.1
  (17 shorter events, 0.2 us)
Async XLA Ops:
  7.2 91.5 %all-gather.3.cloned.1.call-start = ((), (), s32[]{:S(2)}) async-start(), calls=%async_computation | async-start | bytes 2162688 | tf_op jit(solution)/shard_map/all_gather | solution.py:58
  17.5 5.5 %copy-start.2 = (s32[128]{0:T(128)S(1)}, s32[128]{0:T(128)}, u32[]{:S(2)}) copy-start(s32[128]{0:T(128)} %param.11) | copy-start | bytes 1540
  28.5 158.4 %all-gather.5.cloned.1.call-start = ((), (), s32[]{:S(2)}) async-start(), calls=%async_computation.1 | async-start | bytes 2162688 | tf_op jit(solution)/shard_map/all_gather | solution.py:58
  28.8 15.1 %collective-permute-start = (f32[512,64]{1,0:T(8,128)S(1)}, f32[512,64]{1,0:T(8,128)S(1)}, u32[]{:S(2)}, u32[]{:S(2)}) collective-permute-start(f32[512,64]{1,0:T(8,128)S(1)} %squeeze.43), channel_id=1, source_target_pairs={{31,0},{0,1},{1,2},{2,3},{3,4},{4,5},{5,6},{6,7},{7,8},{8,9},{9,10... | collective-permute-start | bytes 393224 | tf_op jit(solution)/shard_map/ppermute | solution.py:13
  29.5 16.6 %collective-permute-start.1 = (f32[512,64]{1,0:T(8,128)S(1)}, f32[512,64]{1,0:T(8,128)S(1)}, u32[]{:S(2)}, u32[]{:S(2)}) collective-permute-start(f32[512,64]{1,0:T(8,128)S(1)} %squeeze.44), channel_id=1, source_target_pairs={{30,0},{31,1},{0,2},{1,3},{2,4},{3,5},{4,6},{5,7},{6,8},{7,9},{8,1... | collective-permute-start | bytes 393224 | tf_op jit(solution)/shard_map/ppermute | solution.py:13
  32.3 23.0 %collective-permute-start.2 = (f32[512,64]{1,0:T(8,128)S(1)}, f32[512,64]{1,0:T(8,128)S(1)}, u32[]{:S(2)}, u32[]{:S(2)}) collective-permute-start(f32[512,64]{1,0:T(8,128)S(1)} %squeeze.45), channel_id=1, source_target_pairs={{29,0},{30,1},{31,2},{0,3},{1,4},{2,5},{3,6},{4,7},{5,8},{6,9},{7,... | collective-permute-start | bytes 393224 | tf_op jit(solution)/shard_map/ppermute | solution.py:13
  34.9 20.4 %collective-permute-start.3 = (f32[512,64]{1,0:T(8,128)S(1)}, f32[512,64]{1,0:T(8,128)S(1)}, u32[]{:S(2)}, u32[]{:S(2)}) collective-permute-start(f32[512,64]{1,0:T(8,128)S(1)} %squeeze.46), channel_id=1, source_target_pairs={{1,0},{2,1},{3,2},{4,3},{5,4},{6,5},{7,6},{8,7},{9,8},{10,9},{11,1... | collective-permute-start | bytes 393224 | tf_op jit(solution)/shard_map/ppermute | solution.py:13
  38.1 19.2 %collective-permute-start.4 = (f32[512,64]{1,0:T(8,128)S(1)}, f32[512,64]{1,0:T(8,128)S(1)}, u32[]{:S(2)}, u32[]{:S(2)}) collective-permute-start(f32[512,64]{1,0:T(8,128)S(1)} %squeeze.47), channel_id=1, source_target_pairs={{2,0},{3,1},{4,2},{5,3},{6,4},{7,5},{8,6},{9,7},{10,8},{11,9},{12,... | collective-permute-start | bytes 393224 | tf_op jit(solution)/shard_map/ppermute | solution.py:13
  44.0 13.3 %collective-permute-start.5 = (f32[512,64]{1,0:T(8,128)}, f32[512,64]{1,0:T(8,128)S(1)}, u32[]{:S(2)}, u32[]{:S(2)}) collective-permute-start(f32[512,64]{1,0:T(8,128)} %squeeze.48), channel_id=1, source_target_pairs={{3,0},{4,1},{5,2},{6,3},{7,4},{8,5},{9,6},{10,7},{11,8},{12,9},{13... | collective-permute-start | bytes 393224 | tf_op jit(solution)/shard_map/ppermute | solution.py:13
  114.2 22.7 %copy-start = (bf16[512,64]{0,1:T(8,128)(2,1)S(1)}, bf16[512,64]{0,1:T(8,128)(2,1)}, u32[]{:S(2)}) copy-start(bf16[512,64]{0,1:T(8,128)(2,1)} %param.7) | copy-start | bytes 196612
  119.9 68.7 %copy-start.1 = (bf16[256,64]{0,1:T(8,128)(2,1)S(1)}, bf16[256,64]{0,1:T(8,128)(2,1)}, u32[]{:S(2)}) copy-start(bf16[256,64]{0,1:T(8,128)(2,1)} %param.8) | copy-start | bytes 98308
  120.1 11.4 %collective-permute-start.10 = (f32[512,64]{1,0:T(8,128)S(1)}, f32[512,64]{1,0:T(8,128)S(1)}, u32[]{:S(2)}, u32[]{:S(2)}) collective-permute-start(f32[512,64]{1,0:T(8,128)S(1)} %squeeze.54), channel_id=1, source_target_pairs={{2,0},{3,1},{4,2},{5,3},{6,4},{7,5},{8,6},{9,7},{10,8},{11,9},{12,... | collective-permute-start | bytes 393224 | tf_op jit(solution)/shard_map/ppermute | solution.py:13
  123.4 14.3 %collective-permute-start.11 = (f32[512,64]{1,0:T(8,128)S(1)}, f32[512,64]{1,0:T(8,128)S(1)}, u32[]{:S(2)}, u32[]{:S(2)}) collective-permute-start(f32[512,64]{1,0:T(8,128)S(1)} %squeeze.55), channel_id=1, source_target_pairs={{3,0},{4,1},{5,2},{6,3},{7,4},{8,5},{9,6},{10,7},{11,8},{12,9},{13... | collective-permute-start | bytes 393224 | tf_op jit(solution)/shard_map/ppermute | solution.py:13
  124.6 13.1 %collective-permute-start.6 = (f32[512,64]{1,0:T(8,128)S(1)}, f32[512,64]{1,0:T(8,128)S(1)}, u32[]{:S(2)}, u32[]{:S(2)}) collective-permute-start(f32[512,64]{1,0:T(8,128)S(1)} %squeeze.50), channel_id=1, source_target_pairs={{31,0},{0,1},{1,2},{2,3},{3,4},{4,5},{5,6},{6,7},{7,8},{8,9},{9,10... | collective-permute-start | bytes 393224 | tf_op jit(solution)/shard_map/ppermute | solution.py:13
  126.1 16.0 %collective-permute-start.7 = (f32[512,64]{1,0:T(8,128)}, f32[512,64]{1,0:T(8,128)S(1)}, u32[]{:S(2)}, u32[]{:S(2)}) collective-permute-start(f32[512,64]{1,0:T(8,128)} %squeeze.51), channel_id=1, source_target_pairs={{30,0},{31,1},{0,2},{1,3},{2,4},{3,5},{4,6},{5,7},{6,8},{7,9},{8,1... | collective-permute-start | bytes 393224 | tf_op jit(solution)/shard_map/ppermute | solution.py:13
  127.6 18.7 %collective-permute-start.8 = (f32[512,64]{1,0:T(8,128)}, f32[512,64]{1,0:T(8,128)S(1)}, u32[]{:S(2)}, u32[]{:S(2)}) collective-permute-start(f32[512,64]{1,0:T(8,128)} %squeeze.52), channel_id=1, source_target_pairs={{29,0},{30,1},{31,2},{0,3},{1,4},{2,5},{3,6},{4,7},{5,8},{6,9},{7,... | collective-permute-start | bytes 393224 | tf_op jit(solution)/shard_map/ppermute | solution.py:13
  131.5 14.8 %collective-permute-start.9 = (f32[512,64]{1,0:T(8,128)}, f32[512,64]{1,0:T(8,128)S(1)}, u32[]{:S(2)}, u32[]{:S(2)}) collective-permute-start(f32[512,64]{1,0:T(8,128)} %squeeze.53), channel_id=1, source_target_pairs={{1,0},{2,1},{3,2},{4,3},{5,4},{6,5},{7,6},{8,7},{9,8},{10,9},{11,1... | collective-permute-start | bytes 393224 | tf_op jit(solution)/shard_map/ppermute | solution.py:13
Sparse Core Ops, SparseCore 0:
  28.6 70.0 all-gather.2
  119.9 66.9 all-gather.4
